TPU v7x, 512 devices: a whole 4x4x16 slice. The times are simulated.
512 devices in a mesh: path: 8 (over y_hi, x), mesh: 2 (over y_lo), grid: 32 (over z, core).
Axes of the slice: x: 4, y: 4 (y_hi: 2, y_lo: 2; y = y_hi * 2 + y_lo), z: 16, core: 2. Of those that a mesh axis runs over, the one named last changes fastest.
Arguments:
- path_bands: float32 [8, 16, 64, 64, 128], P('path', None, 'grid'), may hold values from -6 to 6
- occupied: float32 [2, 1, 64, 64, 128], P('mesh', None, 'grid', 'path'), may hold values from -6 to 6
- path_kpts: int32 [8, 3], P('path'), may hold values from 0 to 7
- mesh_kpts: int32 [2, 3], replicated, may hold values from 0 to 7
- mesh_shift: int32 [2, 3], replicated, may hold values from -1 to 1
Outputs:
- applied: float32 [8, 16, 64, 64, 128], P('path', 'mesh', 'grid')
- intersection: float32 [8, 2, 16, 16], P('path')
All inputs are finite; a program needn't handle non-finite values.
Results may differ from a plain program's by a relative error of at most 0.0001.
Values sent between devices are 32-bit elements; how exact they have to be, the bound alone decides.
A program may use at most 64 MiB of HBM per device.

v0:
```python
import math

import jax
import jax.numpy as jnp
from jax import lax
from jax.sharding import PartitionSpec as P

KDIV = 8


BOX_LENGTH = 42.7
SCREEN_SQ = 0.04
MIXING = 0.25
HIGHEST_PRECISION = lax.Precision.HIGHEST


def in_order(pieces, dim):
    pieces = jnp.moveaxis(pieces, 0, dim)
    lengths = pieces.shape
    return pieces.reshape(*lengths[:dim], lengths[dim] * lengths[dim + 1], *lengths[dim + 2 :])


def from_everyone(array, axis):
    copies = jnp.broadcast_to(array, (lax.axis_size(axis), *array.shape))
    return lax.all_to_all(copies, axis, split_axis=0, concat_axis=0, tiled=True)


def gather_directly(array, axis, dim):
    return in_order(from_everyone(array, axis), dim)


def taken_together(array, axis):
    return from_everyone(array, axis).sum(axis=0)


def signed_frequencies(indices, points):
    return (indices + points // 2) % points - points // 2


def dft_tables(positions, points):
    freqs = jnp.arange(points, dtype=jnp.int32)
    product = positions[:, None] * freqs[None, :] % points
    angles = 2.0 * math.pi / points * product.astype(jnp.float32)
    return (jnp.cos(angles), jnp.sin(angles))


def last_matrix(points, inverse):
    cosine_table, sine_table = dft_tables(jnp.arange(points, dtype=jnp.int32), points)
    if inverse:
        upper = jnp.concatenate([cosine_table, sine_table], 1)
        lower = jnp.concatenate([-sine_table, cosine_table], 1)
    else:
        upper = jnp.concatenate([cosine_table, -sine_table], 1)
        lower = jnp.concatenate([sine_table, cosine_table], 1)
    return jnp.concatenate([upper, lower], 0)


def along_axis(values, cosine_table, sine_table, contract_dim, inverse):
    letters = "abcde"
    form = (
        letters
        + ","
        + letters[contract_dim]
        + "w->"
        + letters[:contract_dim]
        + "w"
        + letters[contract_dim + 1 :]
    )
    cos_part = jnp.einsum(form, values, cosine_table, precision=HIGHEST_PRECISION)
    sin_part = jnp.einsum(form, values, sine_table, precision=HIGHEST_PRECISION)
    half_width = values.shape[-1] // 2
    sin_real = sin_part[..., :half_width]
    sin_imag = sin_part[..., half_width:]
    if inverse:
        return cos_part + jnp.concatenate([-sin_imag, sin_real], -1)
    return cos_part + jnp.concatenate([sin_imag, -sin_real], -1)


def rotate_orbitals(orbitals, shifts, x_planes):
    points = orbitals.shape[3]
    coords = jnp.arange(points, dtype=jnp.int32)
    product = (
        shifts[:, 0][:, None, None, None] * x_planes[None, :, None, None]
        + shifts[:, 1][:, None, None, None] * coords[None, None, :, None]
        + shifts[:, 2][:, None, None, None] * coords[None, None, None, :]
    ) % points
    angles = 2.0 * math.pi / points * product.astype(jnp.float32)
    cosines = jnp.cos(angles)[:, None]
    sines = jnp.sin(angles)[:, None]
    real_part = orbitals[..., :points]
    imag_part = orbitals[..., points:]
    return jnp.concatenate(
        [real_part * cosines - imag_part * sines, real_part * sines + imag_part * cosines], -1
    )


def pair_fields(rotated, band_fields):
    points = band_fields.shape[2]
    rot_real = rotated[..., :points][:, :, None]
    rot_imag = rotated[..., points:][:, :, None]
    band_real = band_fields[..., :points][None, None]
    band_imag = band_fields[..., points:][None, None]
    pairs = jnp.concatenate(
        [rot_real * band_real + rot_imag * band_imag, rot_real * band_imag - rot_imag * band_real],
        -1,
    )
    return pairs.reshape(
        (rotated.shape[0], rotated.shape[1] * band_fields.shape[0]) + band_fields.shape[1:]
    )


def accumulate(rotated, potential, nbands):
    points = rotated.shape[3]
    shaped = potential.reshape((rotated.shape[0], rotated.shape[1], nbands) + potential.shape[2:])
    rot_real = rotated[..., :points][:, :, None]
    rot_imag = rotated[..., points:][:, :, None]
    pot_real = shaped[..., :points]
    pot_imag = shaped[..., points:]
    summed = jnp.concatenate(
        [
            jnp.sum(rot_real * pot_real - rot_imag * pot_imag, axis=(0, 1)),
            jnp.sum(rot_real * pot_imag + rot_imag * pot_real, axis=(0, 1)),
        ],
        -1,
    )
    return -MIXING * summed


def intersection_part(band_fields, applied):
    points = band_fields.shape[2]
    nbands = band_fields.shape[0]
    band_real = band_fields[..., :points].reshape(nbands, -1)
    band_imag = band_fields[..., points:].reshape(nbands, -1)
    app_real = applied[..., :points].reshape(applied.shape[0], -1)
    app_imag = applied[..., points:].reshape(applied.shape[0], -1)
    real_sum = jnp.dot(band_real, app_real.T, precision=HIGHEST_PRECISION) + jnp.dot(
        band_imag, app_imag.T, precision=HIGHEST_PRECISION
    )
    imag_sum = jnp.dot(band_real, app_imag.T, precision=HIGHEST_PRECISION) - jnp.dot(
        band_imag, app_real.T, precision=HIGHEST_PRECISION
    )
    return jnp.stack([real_sum, imag_sum]) / float(points**3)


def screened_kernel(path_point, mesh_points, y_rows, points):
    offset_frac = (path_point[None, :] - mesh_points).astype(jnp.float32) / KDIV
    all_freqs = signed_frequencies(jnp.arange(points, dtype=jnp.int32), points).astype(jnp.float32)
    row_freqs = signed_frequencies(y_rows, points).astype(jnp.float32)
    square_x = (all_freqs[None, :] + offset_frac[:, 0:1]) ** 2
    square_y = (row_freqs[None, :] + offset_frac[:, 1:2]) ** 2
    square_z = (all_freqs[None, :] + offset_frac[:, 2:3]) ** 2
    squares = square_x[:, :, None, None] + square_y[:, None, :, None] + square_z[:, None, None, :]
    kernel = (
        4.0 * math.pi / ((2.0 * math.pi / BOX_LENGTH) ** 2 * squares + SCREEN_SQ) / float(points**3)
    )
    return jnp.concatenate([kernel, kernel], -1)


def per_device(path_bands, occupied, path_kpts, mesh_kpts, mesh_shift):
    points = path_bands.shape[3]
    nbands = path_bands.shape[1]
    local_planes = path_bands.shape[2]
    grid_count = lax.axis_size("grid")
    mesh_count = lax.axis_size("mesh")
    grid_index = lax.axis_index("grid")
    mesh_index = lax.axis_index("mesh")
    whole_orbitals = gather_directly(occupied, "path", 3)
    forward_z = last_matrix(points, False)
    inverse_z = last_matrix(points, True)
    cos_y, sin_y = dft_tables(jnp.arange(points, dtype=jnp.int32), points)
    band_all = path_bands[0]
    path_point = path_kpts[0]
    share_planes = local_planes // mesh_count
    both_orbitals = lax.all_to_all(whole_orbitals, "mesh", split_axis=2, concat_axis=0, tiled=True)
    x_planes = (
        grid_index * local_planes
        + mesh_index * share_planes
        + jnp.arange(share_planes, dtype=jnp.int32)
    )
    rotated = rotate_orbitals(both_orbitals, mesh_shift, x_planes)
    band_mine = lax.dynamic_slice_in_dim(band_all, mesh_index * share_planes, share_planes, 1)
    values = pair_fields(rotated, band_mine)
    values = jnp.matmul(values, forward_z, precision=HIGHEST_PRECISION)
    pair_field = along_axis(values, cos_y, sin_y, 3, False)
    wide_count = mesh_count * grid_count
    rows_y = points // wide_count
    flat_index = mesh_index * grid_count + grid_index
    y_rows = flat_index * rows_y + jnp.arange(rows_y, dtype=jnp.int32)
    kernel = screened_kernel(path_point, mesh_kpts, y_rows, points)
    positions = jnp.arange(points, dtype=jnp.int32)
    piece_index = positions // share_planes
    plane_index = (
        piece_index % grid_count * local_planes
        + piece_index // grid_count * share_planes
        + positions % share_planes
    )
    cos_x, sin_x = dft_tables(plane_index, points)
    moved = (
        along_axis(
            lax.all_to_all(pair_field, ("mesh", "grid"), split_axis=3, concat_axis=2, tiled=True),
            cos_x,
            sin_x,
            2,
            False,
        )
        * kernel[:, None]
    )
    moved = along_axis(moved, cos_x.T, sin_x.T, 2, True)
    potential = lax.all_to_all(moved, ("mesh", "grid"), split_axis=2, concat_axis=3, tiled=True)
    values = potential
    values = along_axis(values, cos_y, sin_y, 3, True)
    applied = accumulate(
        rotated, jnp.matmul(values, inverse_z, precision=HIGHEST_PRECISION), nbands
    )
    partial_value = intersection_part(band_mine, applied)
    result_bands = lax.all_to_all(applied, "mesh", split_axis=0, concat_axis=1, tiled=True)
    intersection = taken_together(partial_value, ("mesh", "grid"))
    return (result_bands[None], intersection[None])


def solution(mesh):
    return jax.shard_map(
        per_device,
        mesh=mesh,
        in_specs=(
            P("path", None, "grid", None, None),
            P("mesh", None, "grid", "path", None),
            P("path", None),
            P(),
            P(),
        ),
        out_specs=(P("path", "mesh", "grid", None, None), P("path", None, None, None)),
        check_vma=False,
    )
```

profile of v0, /device:TPU:1, one launch (start us, length us, event | category | flops | bytes accessed | tf_op | source)
XLA Modules:
  0.0 217.4 jit_solution(2850904999360449276)
XLA Ops:
  0.6 1.4 broadcast_in_dim.8
  2.1 7.5 %all-to-all-start = ((f32[8,1,1,2,8,128]{5,4,3,2,1,0:T(8,128)}), f32[8,1,1,2,8,128]{5,4,3,2,1,0:T(8,128)S(1)}, u32[]{:S(2)}, u32[]{:S(2)}) async-start(f32[8,1,1,2,8,128]{5,4,3,2,1,0:T(8,128)} %broadcast_in_dim.8), calls=%async_computation | async-start | bytes 131072 | tf_op jit(solution)/shard_map/all_to_all | solution.py:25
  9.6 0.3 copy.133
  10.1 0.5 copy-done.1
  11.0 5.2 %all-to-all-done = f32[8,1,1,2,8,128]{5,4,3,2,1,0:T(8,128)S(1)} async-done(((f32[8,1,1,2,8,128]{5,4,3,2,1,0:T(8,128)}), f32[8,1,1,2,8,128]{5,4,3,2,1,0:T(8,128)S(1)}, u32[]{:S(2)}, u32[]{:S(2)}) %all-to-all-start) | async-done | bytes 65568 | tf_op jit(solution)/shard_map/all_to_all | solution.py:25
  16.2 0.6 copy.134
  16.9 3.3 %all-to-all-start.1 = ((f32[1,1,2,64,128]{4,3,1,0,2:T(8,128)}), f32[1,1,2,64,128]{4,3,1,0,2:T(8,128)S(1)}, u32[]{:S(2)}, u32[]{:S(2)}) async-start(f32[1,1,2,64,128]{4,3,1,0,2:T(8,128)} %bitcast.177), calls=%async_computation.1 | async-start | bytes 131072 | tf_op jit(solution)/shard_map/all_to_all | solution.py:174
  20.7 2.5 %all-to-all-done.1 = f32[1,1,2,64,128]{4,3,1,0,2:T(8,128)S(1)} async-done(((f32[1,1,2,64,128]{4,3,1,0,2:T(8,128)}), f32[1,1,2,64,128]{4,3,1,0,2:T(8,128)S(1)}, u32[]{:S(2)}, u32[]{:S(2)}) %all-to-all-start.1) | async-done | bytes 65568 | tf_op jit(solution)/shard_map/all_to_all | solution.py:174
  23.1 0.3 subtract_bitcast_fusion
  23.5 0.3 multiply_add_fusion
  23.8 1.1 fusion.11
  24.9 1.2 convolution_bitcast_fusion.7
  26.0 0.4 fusion.110
  26.4 1.3 fusion
  27.8 1.6 copy.79
  29.4 18.9 %all-to-all-start.2 = ((f32[2,16,1,64,128]{4,1,0,2,3:T(8,128)}), f32[2,16,1,64,128]{4,1,0,2,3:T(8,128)S(1)}, u32[]{:S(2)}, u32[]{:S(2)}) async-start(f32[2,16,1,64,128]{4,1,0,2,3:T(8,128)} %copy.79), calls=%async_computation.2 | async-start | bytes 2097152 | tf_op jit(solution)/shard_map/all_to_all | solution.py:200
  48.4 0.7 copy-done.2
  49.5 49.1 %all-to-all-done.2 = f32[2,16,1,64,128]{4,1,0,2,3:T(8,128)S(1)} async-done(((f32[2,16,1,64,128]{4,1,0,2,3:T(8,128)}), f32[2,16,1,64,128]{4,1,0,2,3:T(8,128)S(1)}, u32[]{:S(2)}, u32[]{:S(2)}) %all-to-all-start.2) | async-done | bytes 1048608 | tf_op jit(solution)/shard_map/all_to_all | solution.py:200
  98.6 1.8 convolution_bitcast_fusion.5
  100.3 0.4 fusion.109
  100.8 2.1 fusion.3
  102.8 1.2 convolution_bitcast_fusion.3
  104.1 0.4 slice_negate_fusion.1
  104.5 1.5 fusion.4
  105.9 0.6 copy.83
  106.6 59.8 %all_to_all.55 = f32[2,16,64,1,128]{4,1,0,3,2:T(8,128)S(1)} all-to-all(f32[2,16,64,1,128]{4,1,0,3,2:T(8,128)S(1)} %copy.83), channel_id=1, replica_groups=mesh['path'=8,'mesh'=2,'grid'=32] {'mesh','grid'}, dimensions={2} | all-to-all | bytes 2097152 | tf_op jit(solution)/shard_map/all_to_all | solution.py:209
  166.3 1.7 convolution_bitcast_fusion.1
  168.0 0.4 slice_negate_fusion
  168.4 1.9 fusion.6
  170.3 1.0 convolution_bitcast_fusion
  171.4 0.4 subtract_reduce_fusion
  171.8 0.3 copy.131
  172.1 0.3 copy.132
  172.6 0.9 convolution_bitcast_fusion.11
  173.5 0.9 convolution_bitcast_fusion.9
  174.4 1.0 copy.89
  175.4 0.8 fusion.8
  176.2 3.5 %all-to-all-start.4 = ((f32[16,1,64,128]{3,2,1,0:T(8,128)}), f32[16,1,64,128]{3,2,1,0:T(8,128)S(1)}, u32[]{:S(2)}, u32[]{:S(2)}) async-start(f32[16,1,64,128]{3,2,1,0:T(8,128)} %copy.89), calls=%async_computation.4 | async-start | bytes 1048576 | tf_op jit(solution)/shard_map/all_to_all | solution.py:216
  179.7 0.9 fusion.10
  180.8 1.0 reshape.472
  181.8 3.3 %all-to-all-done.4 = f32[16,1,64,128]{3,2,1,0:T(8,128)S(1)} async-done(((f32[16,1,64,128]{3,2,1,0:T(8,128)}), f32[16,1,64,128]{3,2,1,0:T(8,128)S(1)}, u32[]{:S(2)}, u32[]{:S(2)}) %all-to-all-start.4) | async-done | bytes 524320 | tf_op jit(solution)/shard_map/all_to_all | solution.py:216
  185.1 12.6 %all-to-all-start.5 = ((f32[64,1,512]{2,1,0:T(1,128)}), f32[64,1,512]{2,1,0:T(1,128)S(1)}, u32[]{:S(2)}, u32[]{:S(2)}) async-start(f32[64,1,512]{2,1,0:T(1,128)} %reshape.472), calls=%async_computation.5 | async-start | bytes 262144 | tf_op jit(solution)/shard_map/all_to_all | solution.py:25
  197.8 0.8 copy.130
  198.6 16.2 %all-to-all-done.5 = f32[64,1,512]{2,1,0:T(1,128)S(1)} async-done(((f32[64,1,512]{2,1,0:T(1,128)}), f32[64,1,512]{2,1,0:T(1,128)S(1)}, u32[]{:S(2)}, u32[]{:S(2)}) %all-to-all-start.5) | async-done | bytes 131104 | tf_op jit(solution)/shard_map/all_to_all | solution.py:25
  214.8 0.5 broadcast.591
  215.4 0.9 reduce.14
  216.3 0.4 reshape.473
  216.7 0.7 reduce_sum.29
  (24 shorter events, 2.0 us)
Async XLA Ops:
  0.6 8.9 %copy-start = (f32[1,16,2,64,128]{4,3,2,1,0:T(8,128)S(1)}, f32[1,16,2,64,128]{4,3,2,1,0:T(8,128)}, u32[]{:S(2)}) copy-start(f32[1,16,2,64,128]{4,3,2,1,0:T(8,128)} %param.5) | copy-start | bytes 3145732
  2.1 14.2 %all-to-all-start = ((f32[8,1,1,2,8,128]{5,4,3,2,1,0:T(8,128)}), f32[8,1,1,2,8,128]{5,4,3,2,1,0:T(8,128)S(1)}, u32[]{:S(2)}, u32[]{:S(2)}) async-start(f32[8,1,1,2,8,128]{5,4,3,2,1,0:T(8,128)} %broadcast_in_dim.8), calls=%async_computation | async-start | bytes 131072 | tf_op jit(solution)/shard_map/all_to_all | solution.py:25
  9.9 0.7 copy-start.1
  16.9 6.3 %all-to-all-start.1 = ((f32[1,1,2,64,128]{4,3,1,0,2:T(8,128)}), f32[1,1,2,64,128]{4,3,1,0,2:T(8,128)S(1)}, u32[]{:S(2)}, u32[]{:S(2)}) async-start(f32[1,1,2,64,128]{4,3,1,0,2:T(8,128)} %bitcast.177), calls=%async_computation.1 | async-start | bytes 131072 | tf_op jit(solution)/shard_map/all_to_all | solution.py:174
  29.4 69.2 %all-to-all-start.2 = ((f32[2,16,1,64,128]{4,1,0,2,3:T(8,128)}), f32[2,16,1,64,128]{4,1,0,2,3:T(8,128)S(1)}, u32[]{:S(2)}, u32[]{:S(2)}) async-start(f32[2,16,1,64,128]{4,1,0,2,3:T(8,128)} %copy.79), calls=%async_computation.2 | async-start | bytes 2097152 | tf_op jit(solution)/shard_map/all_to_all | solution.py:200
  48.3 0.7 copy-start.2
  48.3 0.7 copy-start.3
  176.2 8.9 %all-to-all-start.4 = ((f32[16,1,64,128]{3,2,1,0:T(8,128)}), f32[16,1,64,128]{3,2,1,0:T(8,128)S(1)}, u32[]{:S(2)}, u32[]{:S(2)}) async-start(f32[16,1,64,128]{3,2,1,0:T(8,128)} %copy.89), calls=%async_computation.4 | async-start | bytes 1048576 | tf_op jit(solution)/shard_map/all_to_all | solution.py:216
  185.1 29.7 %all-to-all-start.5 = ((f32[64,1,512]{2,1,0:T(1,128)}), f32[64,1,512]{2,1,0:T(1,128)S(1)}, u32[]{:S(2)}, u32[]{:S(2)}) async-start(f32[64,1,512]{2,1,0:T(1,128)} %reshape.472), calls=%async_computation.5 | async-start | bytes 262144 | tf_op jit(solution)/shard_map/all_to_all | solution.py:25
where the time goes:
time: 218 us; the launch traced here: 217 us
  waiting for transfers between devices  76.3 us (35%)
  blocking collectives  59.8 us (27%)
  starting transfers between devices  45.8 us (21%)
  matrix products  18.2 us (8%)
  local copies, waits for them, and re-layouts  10.8 us (5%)
  other arithmetic  5.5 us (3%)
    all_to_all x1, blocking collectives, per_device(): lax.all_to_all(moved, ('mesh', 'grid'), split_axis=2, concat_axis=3, tile...  59.8 us
    all_to_all x1, waiting for transfers between devices, per_device(): lax.all_to_all(pair_field, ('mesh', 'grid'), split_axis=3, concat_axis=2,...  49.1 us
    all_to_all x2, waiting for transfers between devices, from_everyone(): return lax.all_to_all(copies, axis, split_axis=0, concat_axis=0, tiled=True)  21.5 us
    all_to_all x2, starting transfers between devices, from_everyone(): return lax.all_to_all(copies, axis, split_axis=0, concat_axis=0, tiled=True)  20.1 us
    all_to_all x1, starting transfers between devices, per_device(): lax.all_to_all(pair_field, ('mesh', 'grid'), split_axis=3, concat_axis=2,...  18.9 us
    dot_general x4, matrix products, along_axis(): jnp.einsum(form, values, cosine_table, precision=HIGHEST_PRECISION)  6.76 us
    dot_general x4, matrix products, along_axis(): sin_part = jnp.einsum(form, values, sine_table, precision=HIGHEST_PRECISION)  5.87 us
  transfers between devices with their start and end apart: 5, of which 5 were waited for; matrix products, arithmetic and copies ran while one was open for 2% of the time, Pallas kernels for 0%

commit v1 on v0

v1 whole, which is shorter than its diff:
```python
import functools
import math

import jax
import jax.numpy as jnp
import ml_dtypes
import numpy as np
from jax import lax
from jax.experimental import pallas as pl
from jax.experimental.pallas import tpu as pltpu
from jax.sharding import PartitionSpec as P

KDIV = 8
BOX_LENGTH = 42.7
SCREEN_SQ = 0.04
MIXING = 0.25
MESH = pl.DeviceIdType.MESH
F32 = jnp.float32
BF16 = jnp.bfloat16


def two_terms(table):
    high = table.astype(ml_dtypes.bfloat16)
    low = (table - high.astype(np.float64)).astype(ml_dtypes.bfloat16)
    return high, low


def tables(points):
    half = points // 2
    grid = np.arange(points)
    angles = 2.0 * np.pi / points * (grid[:, None] * grid[None, :] % points)
    cosine, sine = np.cos(angles), np.sin(angles)

    def left(cos_part, sin_part):
        high, low = two_terms(np.concatenate([cos_part, sin_part], 0))
        return np.concatenate([high, high, low, low], 1)

    def right(matrix):
        high, low = two_terms(matrix)
        upper = np.concatenate([high, low], 1)
        lower = np.concatenate([high, np.zeros_like(low)], 1)
        return np.concatenate([upper, lower], 0)

    parts = [slice(0, half), slice(half, points)]
    forward_y = np.stack([left(cosine[part], sine[part]) for part in parts])
    inverse_y = np.stack([left(cosine[:, part], sine[:, part]) for part in parts])
    along_x = left(cosine, sine)
    forward_z = right(np.block([[cosine, -sine], [sine, cosine]]))
    inverse_z = right(np.block([[cosine, sine], [-sine, cosine]]))
    return forward_y, along_x, inverse_y, forward_z, inverse_z


def split(values):
    high = values.astype(BF16)
    return high, (values - high.astype(F32)).astype(BF16)


def body(
    points, nz, npath, nbands,
    kp, km, shift, bands, occ, fy_h, lx_h, iy_h, fz_h, iz_h,
    applied, inter,
    band_full, occ_full, field, part, core_in, y_out, y_in, z_out, z_in, relay_in, mine,
    fy, lx, iy, fz, iz, base, pa, pb, pz, fin,
    loc, oz_s, oz_r, oh_s, oh_r, ox_s, ox_r, oc_s, oc_r,
    bz_s, bz_r, by_s, by_r, bc_s, bc_r, bl_s, bl_r,
    rc_s, rc_r, ry_s, ry_r, rz_s, rz_r, rr_s, rr_r, out_s,
    ia_s, ia_r, ib_s, ib_r, ic_s, ic_r,
):
    width = 2 * points
    half = points // 2
    nx = npath // 2
    rows = points // npath
    share = nbands // 2
    block = nbands // 2

    path = lax.axis_index("path")
    m = lax.axis_index("mesh")
    g = lax.axis_index("grid")
    z = lax.div(g, 2)
    c = lax.rem(g, 2)
    hi_y = lax.div(path, nx)
    at_x = lax.rem(path, nx)
    other_c, other_m = 1 - c, 1 - m
    core_peer = {"grid": 2 * z + other_c}
    y_peer = {"mesh": other_m}
    diag_peer = {"mesh": other_m, "grid": 2 * z + other_c}
    far_path = (1 - hi_y) * nx + at_x
    far_peer = {"path": far_path}

    def x_peer(j):
        return hi_y * nx + lax.rem(at_x + j, nx)

    def offset(i):
        return (nz // 2 - lax.div(i + 1, 2)) * (2 * lax.rem(i, 2) - 1)

    def target(i):
        return lax.rem(z + offset(i) + nz, nz)

    def source(i):
        return lax.rem(z - offset(i) + nz, nz)

    def ring(zz):
        return {"grid": 2 * zz + c}

    def remote(src, dst, send, recv, peer):
        return pltpu.make_async_remote_copy(
            src_ref=src, dst_ref=dst, send_sem=send, recv_sem=recv, device_id=peer, device_id_type=MESH
        )

    def plane(b, j):
        return pl.ds(pl.multiple_of((b * 2 + j) * points, points), points)

    def slab(b):
        return pl.ds(pl.multiple_of(b * points, points), points)

    def path_rows(p):
        return pl.ds(pl.multiple_of(p * rows, rows), rows)

    my_rows = path_rows(path)
    local = [
        pltpu.make_async_copy(occ.at[0, 0], occ_full.at[z, c, :, my_rows, :], loc.at[0]),
        pltpu.make_async_copy(bands.at[plane(z, 0)], band_full.at[z, c, 0], loc.at[1]),
        pltpu.make_async_copy(bands.at[plane(z, 1)], band_full.at[z, c, 1], loc.at[2]),
        pltpu.make_async_copy(fy_h.at[c], fy, loc.at[3]),
        pltpu.make_async_copy(lx_h, lx, loc.at[4]),
        pltpu.make_async_copy(iy_h.at[c], iy, loc.at[5]),
        pltpu.make_async_copy(fz_h, fz, loc.at[6]),
        pltpu.make_async_copy(iz_h, iz, loc.at[7]),
        pltpu.make_async_copy(bands, mine, loc.at[8]),
    ]
    for copy in local:
        copy.start()

    barrier = pltpu.get_barrier_semaphore()

    def greet(i, carry):
        pl.semaphore_signal(barrier, inc=1, device_id=ring(target(i)), device_id_type=MESH)
        return carry

    lax.fori_loop(0, nz - 1, greet, 0)
    for peer in (core_peer, y_peer, diag_peer, far_peer):
        pl.semaphore_signal(barrier, inc=1, device_id=peer, device_id_type=MESH)
    for j in range(1, nx):
        pl.semaphore_signal(barrier, inc=1, device_id={"path": x_peer(j)}, device_id_type=MESH)

    scale = (2.0 * math.pi / BOX_LENGTH) ** 2
    lane = lax.broadcasted_iota(jnp.int32, (points, width), 1)
    row = lax.broadcasted_iota(jnp.int32, (points, width), 0)

    def frequency(index, dim):
        shifted = (index - shift[m, dim] + half) & (points - 1)
        offset_frac = (kp[0, dim] - km[m, dim]).astype(F32) / KDIV
        return (shifted - half).astype(F32) + offset_frac

    freq_x = frequency(row, 0)
    freq_z = frequency(lane & (points - 1), 2)
    base[...] = scale * (freq_x * freq_x + freq_z * freq_z) + SCREEN_SQ

    pl.semaphore_wait(barrier, nz - 1 + 4 + nx - 1)

    def occ_z(i):
        return remote(
            occ.at[0, 0], occ_full.at[z, c, :, my_rows, :], oz_s.at[i], oz_r.at[i], ring(target(i))
        )

    def occ_z_in(i):
        spot = occ_full.at[source(i), c, :, my_rows, :]
        return remote(spot, spot, oz_s.at[i], oz_r.at[i], ring(source(i)))

    def band_z(i):
        dz = target(i)
        return remote(
            bands.at[plane(dz, m)], band_full.at[z, c, m], bz_s.at[i], bz_r.at[i], ring(dz)
        )

    def band_z_in(i):
        spot = band_full.at[source(i), c, m]
        return remote(spot, spot, bz_s.at[i], bz_r.at[i], ring(source(i)))

    def each(count, action):
        def step(i, carry):
            action(i)
            return carry

        lax.fori_loop(0, count, step, 0)

    each(nz - 1, lambda i: occ_z(i).start())
    each(nz - 1, lambda i: band_z(i).start())
    for copy in local[:3]:
        copy.wait()

    def band_own(to_mine):
        spot = band_full.at[z, other_c if to_mine else c]
        return remote(spot, spot, bl_s.at[0], bl_r.at[0], core_peer)

    band_own(False).start()

    def column(cc, p):
        return occ_full.at[:, cc, :, path_rows(p), :]

    def occ_far(p):
        return remote(column(c, p), column(c, p), oh_s.at[0], oh_r.at[0], far_peer)

    def occ_x(j, which, p):
        spot = column(c, p)
        return remote(
            spot, spot, ox_s.at[which, j], ox_r.at[which, j], {"path": x_peer(j)}
        )

    each(nz - 1, lambda i: occ_z_in(i).wait_recv())
    occ_far(path).start()
    for j in range(1, nx):
        occ_x(j, 0, path).start()

    def band_y(i, j):
        spot = band_full.at[source(i), c, j]
        return remote(spot, spot, by_s.at[i], by_r.at[i], y_peer)

    def band_core(i, cc, j, which):
        spot = band_full.at[source(i), cc, j]
        return remote(spot, spot, bc_s.at[which, i], bc_r.at[which, i], core_peer)

    def late(i):
        band_y(i, other_m).wait_recv()
        band_core(i, c, other_m, 1).start()

    def forward(i):
        band_z_in(i).wait_recv()
        band_y(i, m).start()
        band_core(i, c, m, 0).start()
        pl.when(i > 0)(lambda: late(i - 1))

    middle = nz // 2 - 1 if nz > 2 else 0
    each(middle, forward)
    occ_far(far_path).wait_recv()
    for j in range(1, nx):
        occ_x(j, 1, far_path).start()
    lax.fori_loop(middle, nz - 1, lambda i, carry: (forward(i), carry)[1], 0)
    late(nz - 2)
    for j in range(1, nx):
        near = hi_y * nx + lax.rem(at_x - j + nx, nx)
        distant = (1 - hi_y) * nx + lax.rem(at_x - j + nx, nx)
        occ_x(j, 0, near).wait_recv()
        occ_x(j, 1, distant).wait_recv()

    def occ_core(cc):
        spot = occ_full.at[:, cc]
        return remote(spot, spot, oc_s.at[0], oc_r.at[0], core_peer)

    occ_core(c).start()
    for copy in local[3:]:
        copy.wait()
    occ_core(other_c).wait_recv()

    lanes = lax.broadcasted_iota(jnp.int32, (1, width), 1)
    first = lanes < points

    def swap(values):
        return pltpu.roll(values, points, 1)

    def turned(values):
        moved = swap(values)
        return jnp.where(first, moved, -moved)

    def factors(values):
        moved = swap(values)
        return jnp.where(first, values, moved), jnp.where(first, moved, -values)

    def contract(matrix, tiles):
        stacked = jnp.concatenate(tiles, 1) if len(tiles) > 1 else tiles[0]
        high, low = split(stacked)
        right = jnp.concatenate([high, low, high, low], 0)
        out = jnp.dot(matrix, right, preferred_element_type=F32)
        count = out.shape[0] // 2
        return [
            (out[:count, t * width : (t + 1) * width], out[count:, t * width : (t + 1) * width])
            for t in range(len(tiles))
        ]

    def forward_sum(pair):
        return pair[0] + turned(pair[1])

    def inverse_sum(pair):
        return pair[0] - turned(pair[1])

    def along_z(matrix, values):
        high, low = split(values)
        out = jnp.dot(jnp.concatenate([high, low], 1), matrix, preferred_element_type=F32)
        return out[:, :width] + out[:, width:]

    def transform(zz):
        tiles = []
        for cc in range(2):
            for j in range(2):
                band = band_full[zz, cc, j]
                even, odd = factors(occ_full[zz, cc, j])
                tiles.append(even * band + odd * swap(band))
        summed = [forward_sum(pair) for pair in contract(fy[...], tiles)]
        spot = pl.ds(pl.multiple_of(zz * 4 * half, 4 * half), 4 * half)
        field[spot, :] = along_z(fz[...], jnp.concatenate(summed, 0))

    remote_own = band_own(True)
    remote_own.wait_recv()
    transform(z)

    def first_phase(i):
        band_core(i, other_c, m, 0).wait_recv()
        band_core(i, other_c, other_m, 1).wait_recv()
        transform(source(i))

    each(nz - 1, first_phase)

    batch = min(4, half)

    def second_phase(t):
        spots, tiles, kernels = [], [], []
        for k in range(batch):
            gy = t * batch + k
            spots.append(pl.ds(gy, points, stride=half))
            tiles.append(field[spots[k], :])
            freq_y = frequency(c * half + gy, 1)
            kernels.append(
                (-MIXING * 4.0 * math.pi / float(points**3)) / (base[...] + scale * (freq_y * freq_y))
            )
        spectra = [
            forward_sum(pair) * kernel for pair, kernel in zip(contract(lx[...], tiles), kernels)
        ]
        for k, pair in enumerate(contract(lx[...], spectra)):
            field[spots[k], :] = inverse_sum(pair)

    each(half // batch, second_phase)

    def restore(i):
        zz = target(i)
        spot = pl.ds(pl.multiple_of(zz * 4 * half, 4 * half), 4 * half)
        values = along_z(iz[...], field[spot, :])
        tiles = [values[t * half : (t + 1) * half] for t in range(4)]
        for t, pair in enumerate(contract(iy[...], tiles)):
            potential = inverse_sum(pair)
            even, odd = factors(occ_full[zz, t // 2, t % 2])
            part[i, t // 2, t % 2] = even * potential - odd * swap(potential)

    def give_core(i):
        return remote(part.at[i, other_c], core_in.at[i], rc_s.at[i], rc_r.at[i], core_peer)

    def give_y(i):
        return remote(y_out.at[i], y_in.at[i], ry_s.at[i], ry_r.at[i], y_peer)

    def give_z(i):
        return remote(z_out.at[i], z_in.at[slab(z)], rz_s.at[i], rz_r.at[i], ring(target(i)))

    def give_z_in(i):
        spot = z_in.at[slab(source(i))]
        return remote(spot, spot, rz_s.at[i], rz_r.at[i], ring(source(i)))

    def over_cores(i):
        give_core(i).wait_recv()
        y_out[i] = part[i, c, other_m] + core_in[i, other_m]
        z_out[i] = part[i, c, m] + core_in[i, m]

    def over_mesh(i):
        give_y(i).wait_recv()
        total = z_out[i] + y_in[i]
        z_out[i] = total
        pl.when(i == nz - 1)(lambda: keep(total))

    def keep(total):
        z_in[slab(z), :] = total

    lag_core, lag_mesh = 2, 5

    def third_phase(i):
        def at(step, low, high, action):
            pl.when((step >= low) & (step < high))(lambda: action(step))

        at(i - 1, 0, nz, lambda s: give_core(s).start())
        at(i - lag_core - 1, 0, nz, lambda s: give_y(s).start())
        at(i - lag_mesh - 1, 0, nz - 1, lambda s: give_z(s).start())
        at(i, 0, nz, restore)
        at(i - lag_core, 0, nz, over_cores)
        at(i - lag_mesh, 0, nz, over_mesh)

    each(nz + lag_mesh + 1, third_phase)

    def relay(b):
        k = lax.rem(b, share)
        return remote(z_in.at[slab(b)], relay_in.at[slab(k)], rr_s.at[k], rr_r.at[k], y_peer)

    def store(k, own):
        src = z_in.at[slab(m * share + k)] if own else relay_in.at[slab(k)]
        j = m if own else other_m
        return pltpu.make_async_copy(src, applied.at[plane(k, j)], out_s.at[0 if own else 1, k])

    def settle(b):
        owner = lax.div(b, share)
        pl.when(owner == m)(lambda: store(lax.rem(b, share), True).start())
        pl.when(owner != m)(lambda: relay(b).start())

    settle(z)

    def arrive(i):
        give_z_in(i).wait_recv()
        settle(source(i))

    each(nz - 1, arrive)

    def relayed(k):
        relay(other_m * share + k).wait_recv()
        store(k, False).start()

    each(share, relayed)

    chunk = min(16, points)

    def overlap(j, ref, start, total):
        def step(t, total):
            a_tiles, b_tiles = [], []
            for k in range(chunk):
                y = t * chunk + k
                a_tiles.append(mine[pl.ds(j * points + y, nbands, stride=2 * points), :])
                b_tiles.append(ref[pl.ds(start + y, share, stride=points), :])
            a_real = jnp.concatenate(a_tiles, 1)
            a_imag = jnp.concatenate([-turned(tile) for tile in a_tiles], 1)
            b_all = jnp.concatenate(b_tiles, 1)
            zero = jnp.zeros_like(b_all)
            b_all = jnp.concatenate(
                [jnp.where(m == 0, b_all, zero), jnp.where(m == 0, zero, b_all)], 0
            )
            a_high, a_low = split(jnp.concatenate([a_real, a_imag], 0))
            b_high, b_low = split(b_all)
            return total + lax.dot_general(
                jnp.concatenate([a_high, a_low, a_high], 1),
                jnp.concatenate([b_high, b_high, b_low], 1),
                (((1,), (1,)), ((), ())),
                preferred_element_type=F32,
            )

        return lax.fori_loop(0, points // chunk, step, total)

    total = jnp.zeros((2 * nbands, nbands), F32)
    total = overlap(m, z_in, m * share * points, total)
    total = overlap(other_m, relay_in, 0, total)
    pa[...] = jnp.zeros_like(pa)
    total = total * (1.0 / float(points**3))
    for k in range(4):
        pa[k, :, :nbands] = total[k * block : (k + 1) * block]

    quarter = 2 * m + c
    peers = [
        (core_peer, 2 * m + other_c),
        (y_peer, 2 * other_m + c),
        (diag_peer, 2 * other_m + other_c),
    ]

    def gather_pair(k):
        return remote(pa.at[peers[k][1]], pb.at[k], ia_s.at[k], ia_r.at[k], peers[k][0])

    for k in range(3):
        gather_pair(k).start()
    for k in range(3):
        gather_pair(k).wait_recv()
    pz[z] = (pa[quarter] + pb[0]) + (pb[1] + pb[2])

    def sum_z(i):
        return remote(pz.at[z], pz.at[z], ib_s.at[i], ib_r.at[i], ring(target(i)))

    def sum_z_in(i):
        spot = pz.at[source(i)]
        return remote(spot, spot, ib_s.at[i], ib_r.at[i], ring(source(i)))

    each(nz - 1, lambda i: sum_z(i).start())
    each(nz - 1, lambda i: sum_z_in(i).wait_recv())
    whole = pz[0]
    for k in range(1, nz):
        whole = whole + pz[k]
    fin[quarter] = whole

    def spread(k, into):
        spot = fin.at[into]
        return remote(spot, spot, ic_s.at[k], ic_r.at[k], peers[k][0])

    for k in range(3):
        spread(k, quarter).start()
    for k in range(3):
        spread(k, peers[k][1]).wait_recv()
    for k in range(4):
        inter[k * block : (k + 1) * block, :] = fin[k, :, :nbands]

    each(nz - 1, lambda i: occ_z(i).wait_send())
    each(nz - 1, lambda i: band_z(i).wait_send())
    band_own(False).wait_send()
    occ_far(path).wait_send()
    for j in range(1, nx):
        occ_x(j, 0, path).wait_send()
        occ_x(j, 1, far_path).wait_send()
    occ_core(c).wait_send()
    each(nz - 1, lambda i: band_y(i, m).wait_send())
    each(nz - 1, lambda i: band_core(i, c, m, 0).wait_send())
    each(nz - 1, lambda i: band_core(i, c, other_m, 1).wait_send())
    each(nz, lambda i: give_core(i).wait_send())
    each(nz, lambda i: give_y(i).wait_send())
    each(nz - 1, lambda i: give_z(i).wait_send())
    each(share, lambda k: relay(other_m * share + k).wait_send())
    each(share, lambda k: store(k, True).wait())
    each(share, lambda k: store(k, False).wait())
    for k in range(3):
        gather_pair(k).wait_send()
        spread(k, quarter).wait_send()
    each(nz - 1, lambda i: sum_z(i).wait_send())


def per_device(path_bands, occupied, path_kpts, mesh_kpts, mesh_shift):
    nbands, planes, points, width = path_bands.shape[1:]
    npath = lax.axis_size("path")
    nz = lax.axis_size("grid") // 2
    assert planes == 2 and nz == nbands and lax.axis_size("mesh") == 2
    half = points // 2
    share = nbands // 2
    forward_y, along_x, inverse_y, forward_z, inverse_z = tables(points)
    smem = pl.BlockSpec(memory_space=pltpu.SMEM)
    anywhere = pl.BlockSpec(memory_space=pl.ANY)
    vmem = lambda *shape: pltpu.VMEM(shape, F32)
    table = lambda array: pltpu.VMEM(array.shape, BF16)
    dma = lambda *shape: pltpu.SemaphoreType.DMA(shape)
    block = 2 * nbands // 4
    pairs = lambda *shape: [dma(*shape), dma(*shape)]
    scratch = [
        vmem(nz, 2, 2, points, width),
        vmem(nz, 2, 2, points, width),
        vmem(points * half, width),
        vmem(nz, 2, 2, points, width),
        vmem(nz, 2, points, width),
        vmem(nz, points, width),
        vmem(nz, points, width),
        vmem(nz, points, width),
        vmem(nbands * points, width),
        vmem(share * points, width),
        vmem(nbands * 2 * points, width),
        table(forward_y[0]),
        table(along_x),
        table(inverse_y[0]),
        table(forward_z),
        table(inverse_z),
        vmem(points, width),
        vmem(4, block, 128),
        vmem(3, block, 128),
        vmem(nz, block, 128),
        vmem(4, block, 128),
        dma(9),
        *pairs(nz),
        *pairs(1),
        *pairs(2, max(npath // 2, 1)),
        *pairs(1),
        *pairs(nz),
        *pairs(nz),
        *pairs(2, nz),
        *pairs(1),
        *pairs(nz),
        *pairs(nz),
        *pairs(nz),
        *pairs(share),
        dma(2, share),
        *pairs(3),
        *pairs(nz),
        *pairs(3),
    ]
    applied, inter = pl.pallas_call(
        functools.partial(body, points, nz, npath, nbands),
        name="exchange",
        out_shape=(
            jax.ShapeDtypeStruct((share * 2 * points, width), F32),
            jax.ShapeDtypeStruct((2 * nbands, nbands), F32),
        ),
        in_specs=[smem] * 3 + [anywhere] * 7,
        out_specs=(anywhere, pl.BlockSpec(memory_space=pltpu.VMEM)),
        scratch_shapes=scratch,
        compiler_params=pltpu.CompilerParams(
            collective_id=0, has_side_effects=True, vmem_limit_bytes=40 << 20
        ),
    )(
        path_kpts,
        mesh_kpts,
        mesh_shift,
        path_bands.reshape(nbands * planes * points, width),
        occupied,
        jnp.asarray(forward_y),
        jnp.asarray(along_x),
        jnp.asarray(inverse_y),
        jnp.asarray(forward_z),
        jnp.asarray(inverse_z),
    )
    return (
        applied.reshape(1, share, planes, points, width),
        inter.reshape(1, 2, nbands, nbands),
    )


def solution(mesh):
    return jax.shard_map(
        per_device,
        mesh=mesh,
        in_specs=(
            P("path", None, "grid", None, None),
            P("mesh", None, "grid", "path", None),
            P("path", None),
            P(),
            P(),
        ),
        out_specs=(P("path", "mesh", "grid", None, None), P("path", None, None, None)),
        check_vma=False,
    )
```

time: 218 us -> 139 us (0.64)
  Pallas kernels: 0 us -> 129 us
  waiting for transfers between devices: 76.3 us -> 0 us
  blocking collectives: 59.8 us -> 0 us
  starting transfers between devices: 45.8 us -> 0 us
  matrix products: 18.2 us -> 0 us
  other arithmetic: 5.5 us -> 0 us
    pallas_call x0 -> x1, Pallas kernels: none -> 129 us  [per_device(): pl.pallas_call(functools.partial(body, points, nz, npath, nbands), name='...]
    all_to_all x5 -> x0, waiting for transfers between devices: 76.3 us -> none  [the longest x1 49.1 us: per_device(): lax.all_to_all(pair_field, ('mesh', 'grid'), split_axis=3, concat_axis=2,...]
    all_to_all x1 -> x0, blocking collectives: 59.8 us -> none  [per_device(): lax.all_to_all(moved, ('mesh', 'grid'), split_axis=2, concat_axis=3, tile...]
    all_to_all x5 -> x0, starting transfers between devices: 45.8 us -> none  [the longest x2 20.1 us: from_everyone(): return lax.all_to_all(copies, axis, split_axis=0, concat_axis=0, tiled=True)]
    dot_general x14 -> x0, matrix products: 18.2 us -> none  [the longest x4 6.76 us: along_axis(): jnp.einsum(form, values, cosine_table, precision=HIGHEST_PRECISION)]
    unnamed x10 -> x22, local copies, waits for them, and re-layouts: 2.54 us -> 8.99 us
    add x2 -> x0, local copies, waits for them, and re-layouts: 2.21 us -> none  [the longest x1 1.6 us: along_axis(): return cos_part + jnp.concatenate([sin_imag, -sin_real], -1)]
  transfers between devices with their start and end apart: 5 -> 0, of which waited for: 5 -> 0; matrix products, arithmetic and copies ran while one was open for 2% -> 0% of each run, Pallas kernels for 0% -> 0%
where the time goes in v1:
time: 139 us
  Pallas kernels  129 us (93%)
  local copies, waits for them, and re-layouts  8.99 us (6%)
    pallas_call x1, Pallas kernels, per_device(): pl.pallas_call(functools.partial(body, points, nz, npath, nbands), name='...  129 us
    unnamed x22, local copies, waits for them, and re-layouts  8.99 us

profile of v1, /device:TPU:1, one launch (start us, length us, event | category | flops | bytes accessed | tf_op | source)
XLA Modules:
  0.0 138.8 jit_solution(11289289811893492981)
XLA Ops:
  0.6 0.0 copy-start.7
  0.6 0.0 copy-start.9
  0.7 0.7 copy-done.7
  1.3 0.0 copy-done.9
  1.3 0.0 copy-start
  1.3 1.2 copy-done
  2.5 0.0 copy-start.1
  2.5 0.9 copy-done.1
  3.4 0.0 copy-start.2
  3.4 0.9 copy-done.2
  4.3 0.0 copy-start.3
  4.4 0.8 copy-done.3
  5.2 0.0 copy-start.4
  5.2 0.8 copy-done.4
  6.0 0.0 copy-start.5
  6.0 0.8 copy-done.5
  6.9 0.0 copy-start.6
  6.9 0.7 copy-done.6
  7.6 0.0 copy-start.8
  7.6 0.7 copy-done.8
  8.2 129.2 %exchange.1 = (f32[1024,128]{1,0:T(8,128)S(1)}, f32[32,16]{1,0:T(8,128)S(1)}) custom-call(s32[1,3]{1,0:T(1,128)S(1)} %copy-done.9, s32[2,3]{1,0:T(2,128)S(1)} %copy-done.7, s32[2,3]{1,0:T(2,128)S(1)} %copy-done.8, f32[2048,128]{1,0:T(8,128)S(1)} %bitcast.3, f32[1,1,2,8,128]{4,3,2,1,0:T(8,128)S(1)} %copy-done.6, bf16[2,64,256]{2,1,0:T(8,128)(2,1)S(1)} %copy-done.5, ...), custom_call_target="tpu_custom_call" | custom-call | tf_op jit(solution)/shard_map/exchange/pallas_call | solution.py:567
  137.4 0.8 copy.14
  138.2 0.6 copy.15
Async XLA Ops:
  0.6 0.7 copy-start.7
  0.6 0.7 copy-start.9
  1.3 1.2 copy-start
  2.5 0.9 copy-start.1
  3.4 0.9 copy-start.2
  4.3 0.8 copy-start.3
  5.2 0.8 copy-start.4
  6.0 0.8 copy-start.5
  6.9 0.7 copy-start.6
  7.6 0.7 copy-start.8

commit v2 on v1

v2 whole, which is shorter than its diff:
```python
import functools
import math

import jax
import jax.numpy as jnp
import ml_dtypes
import numpy as np
from jax import lax
from jax.experimental import pallas as pl
from jax.experimental.pallas import tpu as pltpu
from jax.sharding import PartitionSpec as P

KDIV = 8
BOX_LENGTH = 42.7
SCREEN_SQ = 0.04
MIXING = 0.25
MESH = pl.DeviceIdType.MESH
F32 = jnp.float32
BF16 = jnp.bfloat16


def two_terms(table):
    high = table.astype(ml_dtypes.bfloat16)
    low = (table - high.astype(np.float64)).astype(ml_dtypes.bfloat16)
    return high, low


def tables(points):
    half = points // 2
    grid = np.arange(points)
    angles = 2.0 * np.pi / points * (grid[:, None] * grid[None, :] % points)
    cosine, sine = np.cos(angles), np.sin(angles)

    def left(cos_part, sin_part):
        high, low = two_terms(np.concatenate([cos_part, sin_part], 0))
        return np.concatenate([high, high, low, low], 1)

    def right(matrix):
        high, low = two_terms(matrix)
        upper = np.concatenate([high, low], 1)
        lower = np.concatenate([high, np.zeros_like(low)], 1)
        return np.concatenate([upper, lower], 0)

    parts = [slice(0, half), slice(half, points)]
    forward_y = np.stack([left(cosine[part], sine[part]) for part in parts])
    inverse_y = np.stack([left(cosine[:, part], sine[:, part]) for part in parts])
    along_x = left(cosine, sine)
    forward_z = right(np.block([[cosine, -sine], [sine, cosine]]))
    inverse_z = right(np.block([[cosine, sine], [-sine, cosine]]))
    return forward_y, along_x, inverse_y, forward_z, inverse_z


def split(values):
    high = values.astype(BF16)
    return high, (values - high.astype(F32)).astype(BF16)


def layout(points, nz):
    near_count = {16: 4}.get(nz, 2)
    return nz // near_count, near_count, points // 2 + 8


def body(
    points, nz, npath, nbands,
    kp_h, km_h, shift_h, bands, occ, fy_h, lx_h, iy_h, fz_h, iz_h,
    applied, inter,
    band_full, occ_full, field, part, core_in, y_out, y_in, z_out, z_in, relay_in, mine,
    fy, lx, iy, fz, iz, base, acc, pz, fin, kp, km, shift,
    loc, of_s, of_r, on_s, on_r, oh_s, oh_r, ox_s, ox_r, oc_s, oc_r,
    bz_s, bz_r, by_s, by_r, bc_s, bc_r, bl_s, bl_r,
    rc_s, rc_r, ry_s, ry_r, rz_s, rz_r, rr_s, rr_r, out_s,
    ib_s, ib_r, ic_s, ic_r,
):
    width = 2 * points
    half = points // 2
    nx = npath // 2
    rows = points // npath
    share = nbands // 2
    block = nbands // 2
    far_count, near_count, pitch = layout(points, nz)

    path = lax.axis_index("path")
    m = lax.axis_index("mesh")
    g = lax.axis_index("grid")
    z = lax.div(g, 2)
    c = lax.rem(g, 2)
    hi_y = lax.div(path, nx)
    at_x = lax.rem(path, nx)
    other_c, other_m = 1 - c, 1 - m
    core_peer = {"grid": 2 * z + other_c}
    y_peer = {"mesh": other_m}
    diag_peer = {"mesh": other_m, "grid": 2 * z + other_c}
    far_path = (1 - hi_y) * nx + at_x
    far_peer = {"path": far_path}

    def x_peer(j):
        return hi_y * nx + lax.rem(at_x + j, nx)

    def offset(i):
        return (lax.div(i, 2) + 1) * (1 - 2 * lax.rem(i, 2)) * jnp.where(i == nz - 1, 0, 1)

    def target(i):
        return lax.rem(z + offset(i) + nz, nz)

    def source(i):
        return lax.rem(z - offset(i) + nz, nz)

    def ring(zz):
        return {"grid": 2 * zz + c}

    def remote(src, dst, send, recv, peer):
        return pltpu.make_async_remote_copy(
            src_ref=src, dst_ref=dst, send_sem=send, recv_sem=recv, device_id=peer, device_id_type=MESH
        )

    def plane(b, j):
        return pl.ds(pl.multiple_of((b * 2 + j) * points, points), points)

    def slab(b):
        return pl.ds(pl.multiple_of(b * points, points), points)

    def path_rows(p):
        return pl.ds(pl.multiple_of(p * rows, rows), rows)

    my_rows = path_rows(path)
    far, near = lax.div(z, near_count), lax.rem(z, near_count)
    local = [
        pltpu.make_async_copy(occ.at[0, 0], occ_full.at[far, near, c, :, my_rows, :], loc.at[0]),
        pltpu.make_async_copy(bands.at[plane(z, 0)], band_full.at[z, c, 0], loc.at[1]),
        pltpu.make_async_copy(bands.at[plane(z, 1)], band_full.at[z, c, 1], loc.at[2]),
        pltpu.make_async_copy(fy_h.at[c], fy, loc.at[3]),
        pltpu.make_async_copy(lx_h, lx, loc.at[4]),
        pltpu.make_async_copy(iy_h.at[c], iy, loc.at[5]),
        pltpu.make_async_copy(fz_h, fz, loc.at[6]),
        pltpu.make_async_copy(iz_h, iz, loc.at[7]),
        pltpu.make_async_copy(kp_h, kp, loc.at[8]),
        pltpu.make_async_copy(km_h, km, loc.at[9]),
        pltpu.make_async_copy(shift_h, shift, loc.at[10]),
        pltpu.make_async_copy(bands, mine, loc.at[11]),
    ]
    for copy in local:
        copy.start()

    barrier = pltpu.get_barrier_semaphore()

    def greet(i, carry):
        pl.semaphore_signal(barrier, inc=1, device_id=ring(target(i)), device_id_type=MESH)
        return carry

    lax.fori_loop(0, nz - 1, greet, 0)
    for peer in (core_peer, y_peer, diag_peer, far_peer):
        pl.semaphore_signal(barrier, inc=1, device_id=peer, device_id_type=MESH)
    for j in range(1, nx):
        pl.semaphore_signal(barrier, inc=1, device_id={"path": x_peer(j)}, device_id_type=MESH)

    pl.semaphore_wait(barrier, nz - 1 + 4 + nx - 1)

    def each(low, high, action):
        def step(i, carry):
            action(i)
            return carry

        lax.fori_loop(low, high, step, 0)

    near_steps = [(1, -1, 2)[e] for e in range(near_count - 1)]

    def occ_far_z(k, back=False):
        at = lax.rem(far + (far_count - k if back else k), far_count)
        spot = occ_full.at[at if back else far, near, c, :, my_rows, :]
        src = spot if back else occ.at[0, 0]
        return remote(src, spot, of_s.at[k], of_r.at[k], ring(at * near_count + near))

    def occ_near_z(k, back=False):
        step = near_steps[k]
        zz = lax.rem(z + nz - step if back else z + nz + step, nz)
        spot = occ_full.at[:, lax.rem(zz, near_count) if back else near, c, :, my_rows, :]
        return remote(spot, spot, on_s.at[k], on_r.at[k], ring(zz))

    def band_z(i):
        dz = target(i)
        return remote(
            bands.at[plane(dz, m)], band_full.at[z, c, m], bz_s.at[i], bz_r.at[i], ring(dz)
        )

    def band_z_in(i):
        spot = band_full.at[source(i), c, m]
        return remote(spot, spot, bz_s.at[i], bz_r.at[i], ring(source(i)))

    def band_own(to_mine):
        spot = band_full.at[z, other_c if to_mine else c]
        return remote(spot, spot, bl_s.at[0], bl_r.at[0], core_peer)

    def column(cc, p):
        return occ_full.at[:, :, cc, :, path_rows(p), :]

    def occ_far(p):
        return remote(column(c, p), column(c, p), oh_s.at[0], oh_r.at[0], far_peer)

    def occ_x(j, which, p):
        spot = column(c, p)
        return remote(
            spot, spot, ox_s.at[which, j], ox_r.at[which, j], {"path": x_peer(j)}
        )

    def occ_core(cc, p):
        spot = column(cc, p)
        return remote(spot, spot, oc_s.at[p], oc_r.at[p], core_peer)

    def band_y(i, j):
        spot = band_full.at[source(i), c, j]
        return remote(spot, spot, by_s.at[i], by_r.at[i], y_peer)

    def band_core(i, cc, j, which):
        spot = band_full.at[source(i), cc, j]
        return remote(spot, spot, bc_s.at[which, i], bc_r.at[which, i], core_peer)

    def late(i):
        band_y(i, other_m).wait_recv()
        band_core(i, c, other_m, 1).start()

    def forward(i):
        band_z_in(i).wait_recv()
        band_y(i, m).start()
        band_core(i, c, m, 0).start()
        pl.when(i > 0)(lambda: late(i - 1))

    steps = nz - 1
    first_stop, second_stop, third_stop, fourth_stop = (
        (4, 8, 9, 10) if nz == 16 else (1, steps, steps, steps)
    )
    for k in range(1, far_count):
        occ_far_z(k).start()
    each(0, second_stop, lambda i: band_z(i).start())
    for copy in local[:3]:
        copy.wait()
    band_own(False).start()
    each(0, first_stop, forward)
    for k in range(1, far_count):
        occ_far_z(k, True).wait_recv()
    for k in range(near_count - 1):
        occ_near_z(k).start()
    each(second_stop, steps, lambda i: band_z(i).start())
    for copy in local[3:]:
        copy.wait()

    scale = (2.0 * math.pi / BOX_LENGTH) ** 2
    lane = lax.broadcasted_iota(jnp.int32, (points, width), 1)
    row = lax.broadcasted_iota(jnp.int32, (points, width), 0)

    def frequency(index, dim):
        shifted = (index - shift[m, dim] + half) & (points - 1)
        offset_frac = (kp[0, dim] - km[m, dim]).astype(F32) / KDIV
        return (shifted - half).astype(F32) + offset_frac

    freq_x = frequency(row, 0)
    freq_z = frequency(lane & (points - 1), 2)
    base[...] = scale * (freq_x * freq_x + freq_z * freq_z) + SCREEN_SQ

    for k in range(near_count - 1):
        occ_near_z(k, True).wait_recv()
    occ_far(path).start()
    for j in range(1, nx):
        occ_x(j, 0, path).start()
    occ_core(c, path).start()
    each(first_stop, third_stop, forward)
    occ_far(far_path).wait_recv()
    for j in range(1, nx):
        occ_x(j, 1, far_path).start()
    occ_core(c, far_path).start()
    each(third_stop, fourth_stop, forward)
    for which in range(2):
        for j in range(1, nx):
            side = hi_y if which == 0 else 1 - hi_y
            p = side * nx + lax.rem(at_x - j + nx, nx)
            occ_x(j, which, p).wait_recv()
            occ_core(c, p).start()
    each(0, npath, lambda p: occ_core(other_c, p).wait_recv())

    lanes = lax.broadcasted_iota(jnp.int32, (1, width), 1)
    first = lanes < points

    def swap(values):
        return pltpu.roll(values, points, 1)

    def turned(values):
        moved = swap(values)
        return jnp.where(first, moved, -moved)

    def factors(values):
        moved = swap(values)
        return jnp.where(first, values, moved), jnp.where(first, moved, -values)

    def contract(matrix, tiles):
        stacked = jnp.concatenate(tiles, 1) if len(tiles) > 1 else tiles[0]
        high, low = split(stacked)
        right = jnp.concatenate([high, low, high, low], 0)
        out = jnp.dot(matrix, right, preferred_element_type=F32)
        count = out.shape[0] // 2
        return [
            (out[:count, t * width : (t + 1) * width], out[count:, t * width : (t + 1) * width])
            for t in range(len(tiles))
        ]

    def forward_sum(pair):
        return pair[0] + turned(pair[1])

    def inverse_sum(pair):
        return pair[0] - turned(pair[1])

    def along_z(matrix, values):
        high, low = split(values)
        out = jnp.dot(jnp.concatenate([high, low], 1), matrix, preferred_element_type=F32)
        return out[:, :width] + out[:, width:]

    def orbital(zz, cc, j):
        return occ_full[lax.div(zz, near_count), lax.rem(zz, near_count), cc, j]

    def x_rows(zz, t):
        return pl.ds(pl.multiple_of((zz * 4 + t) * pitch, 8), half)

    def transform(zz):
        tiles = []
        for t in range(4):
            band = band_full[zz, t // 2, t % 2]
            even, odd = factors(orbital(zz, t // 2, t % 2))
            tiles.append(even * band + odd * swap(band))
        summed = [forward_sum(pair) for pair in contract(fy[...], tiles)]
        values = along_z(fz[...], jnp.concatenate(summed, 0))
        for t in range(4):
            field[x_rows(zz, t), :] = values[t * half : (t + 1) * half]

    def first_phase(t):
        step = fourth_stop + lax.div(t, 3)
        turn = lax.rem(t, 3) == 0
        pl.when(turn & (step < steps))(lambda: forward(step))
        pl.when(turn & (step == steps))(lambda: late(steps - 1))

        def fetched():
            band_core(t - 1, other_c, m, 0).wait_recv()
            band_core(t - 1, other_c, other_m, 1).wait_recv()

        pl.when(t > 0)(fetched)
        pl.when(t == 0)(lambda: band_own(True).wait_recv())
        transform(source(jnp.where(t == 0, nz - 1, t - 1)))

    each(0, nz, first_phase)

    batch = min(4, half)

    def second_phase(t):
        spots, tiles, kernels = [], [], []
        for k in range(batch):
            gy = t * batch + k
            spots.append(pl.ds(gy, points, stride=pitch))
            tiles.append(field[spots[k], :])
            freq_y = frequency(c * half + gy, 1)
            kernels.append(
                (-MIXING * 4.0 * math.pi / float(points**3)) / (base[...] + scale * (freq_y * freq_y))
            )
        spectra = [
            forward_sum(pair) * kernel for pair, kernel in zip(contract(lx[...], tiles), kernels)
        ]
        for k, pair in enumerate(contract(lx[...], spectra)):
            field[spots[k], :] = inverse_sum(pair)

    each(0, half // batch, second_phase)

    def restore(i):
        zz = target(i)
        values = along_z(
            iz[...], jnp.concatenate([field[x_rows(zz, t), :] for t in range(4)], 0)
        )
        tiles = [values[t * half : (t + 1) * half] for t in range(4)]
        for t, pair in enumerate(contract(iy[...], tiles)):
            potential = inverse_sum(pair)
            even, odd = factors(orbital(zz, t // 2, t % 2))
            part[i, t // 2, t % 2] = even * potential - odd * swap(potential)

    def give_core(i):
        return remote(part.at[i, other_c], core_in.at[i], rc_s.at[i], rc_r.at[i], core_peer)

    def give_y(i):
        return remote(y_out.at[i], y_in.at[i], ry_s.at[i], ry_r.at[i], y_peer)

    def give_z(i):
        return remote(z_out.at[i], z_in.at[slab(z)], rz_s.at[i], rz_r.at[i], ring(target(i)))

    def give_z_in(i):
        spot = z_in.at[slab(source(i))]
        return remote(spot, spot, rz_s.at[i], rz_r.at[i], ring(source(i)))

    def over_cores(i):
        give_core(i).wait_recv()
        y_out[i] = part[i, c, other_m] + core_in[i, other_m]
        z_out[i] = part[i, c, m] + core_in[i, m]

    def over_mesh(i):
        give_y(i).wait_recv()
        total = z_out[i] + y_in[i]
        z_out[i] = total
        pl.when(i == nz - 1)(lambda: keep(total))

    def keep(total):
        z_in[slab(z), :] = total

    lag_core, lag_mesh = 2, 5

    def third_phase(i):
        def at(step, low, high, action):
            pl.when((step >= low) & (step < high))(lambda: action(step))

        at(i - 1, 0, nz, lambda s: give_core(s).start())
        at(i - lag_core - 1, 0, nz, lambda s: give_y(s).start())
        at(i - lag_mesh - 1, 0, nz - 1, lambda s: give_z(s).start())
        at(i, 0, nz, restore)
        at(i - lag_core, 0, nz, over_cores)
        at(i - lag_mesh, 0, nz, over_mesh)

    each(0, nz + lag_mesh + 1, third_phase)

    def relay(b):
        k = lax.rem(b, share)
        return remote(z_in.at[slab(b)], relay_in.at[slab(k)], rr_s.at[k], rr_r.at[k], y_peer)

    def store(k, own):
        src = z_in.at[slab(m * share + k)] if own else relay_in.at[slab(k)]
        j = m if own else other_m
        return pltpu.make_async_copy(src, applied.at[plane(k, j)], out_s.at[0 if own else 1, k])

    def overlap(k, j, values, fresh):
        other = turned(values)
        sums = []
        for factor in (values, other):
            for a in range(nbands):
                sums.append(jnp.sum(mine[plane(a, j), :] * factor, axis=0, keepdims=True))
        total = jnp.concatenate(sums, 0)
        acc[k] = total if fresh else acc[k] + total

    def settle(b):
        owner, k = lax.div(b, share), lax.rem(b, share)

        def own():
            store(k, True).start()
            overlap(k, m, z_in[slab(b), :], True)

        pl.when(owner == m)(own)
        pl.when(owner != m)(lambda: relay(b).start())

    def relayed(b):
        def own():
            k = lax.rem(b, share)
            relay(other_m * share + k).wait_recv()
            store(k, False).start()
            overlap(k, other_m, relay_in[slab(k), :], False)

        pl.when(lax.div(b, share) == m)(own)

    def arrive(i):
        pl.when(i > 0)(lambda: give_z_in(i - 1).wait_recv())
        pl.when(i < nz)(lambda: settle(source(jnp.where(i == 0, nz - 1, i - 1))))

    lag_relay = 2

    def arrive_step(i):
        pl.when(i < nz)(lambda: arrive(i))
        before = i - lag_relay
        pl.when(before >= 0)(
            lambda: relayed(source(jnp.where(before == 0, nz - 1, before - 1)))
        )

    each(0, nz + lag_relay, arrive_step)

    tile = jnp.zeros((block, 128), F32)
    tile_lane = lax.broadcasted_iota(jnp.int32, (block, 128), 1)
    for k in range(share):
        rows_of = acc[k]
        for group in range(4):
            column_sum = jnp.sum(
                rows_of[group * block : (group + 1) * block], axis=1, keepdims=True
            )
            here = tile_lane == group * nbands + share * m + k
            tile = tile + jnp.where(here, column_sum, 0.0)
    pz[z] = tile * (1.0 / float(points**3))

    def sum_z(i):
        return remote(pz.at[z], pz.at[z], ib_s.at[i], ib_r.at[i], ring(target(i)))

    def sum_z_in(i):
        spot = pz.at[source(i)]
        return remote(spot, spot, ib_s.at[i], ib_r.at[i], ring(source(i)))

    each(0, steps, lambda i: sum_z(steps - 1 - i).start())
    each(0, steps, lambda i: sum_z_in(i).wait_recv())
    whole = pz[0]
    for k in range(1, nz):
        whole = whole + pz[k]
    quarter = 2 * m + c
    fin[quarter] = whole
    peers = [
        (core_peer, 2 * m + other_c),
        (y_peer, 2 * other_m + c),
        (diag_peer, 2 * other_m + other_c),
    ]

    def spread(k, into):
        spot = fin.at[into]
        return remote(spot, spot, ic_s.at[k], ic_r.at[k], peers[k][0])

    for k in range(3):
        spread(k, quarter).start()
    for k in range(3):
        spread(k, peers[k][1]).wait_recv()
    result = (fin[0] + fin[1]) + (fin[2] + fin[3])
    for group in range(4):
        turned_tile = result if group == 0 else pltpu.roll(result, 128 - group * nbands, 1)
        inter[group * block : (group + 1) * block, :] = turned_tile[:, :nbands]

    for k in range(1, far_count):
        occ_far_z(k).wait_send()
    for k in range(near_count - 1):
        occ_near_z(k).wait_send()
    each(0, steps, lambda i: band_z(i).wait_send())
    band_own(False).wait_send()
    occ_far(path).wait_send()
    for j in range(1, nx):
        occ_x(j, 0, path).wait_send()
        occ_x(j, 1, far_path).wait_send()
    each(0, npath, lambda p: occ_core(c, p).wait_send())
    each(0, steps, lambda i: band_y(i, m).wait_send())
    each(0, steps, lambda i: band_core(i, c, m, 0).wait_send())
    each(0, steps, lambda i: band_core(i, c, other_m, 1).wait_send())
    each(0, nz, lambda i: give_core(i).wait_send())
    each(0, nz, lambda i: give_y(i).wait_send())
    each(0, steps, lambda i: give_z(i).wait_send())
    each(0, share, lambda k: relay(other_m * share + k).wait_send())
    each(0, share, lambda k: store(k, True).wait())
    each(0, share, lambda k: store(k, False).wait())
    for k in range(3):
        spread(k, quarter).wait_send()
    each(0, steps, lambda i: sum_z(i).wait_send())


def per_device(path_bands, occupied, path_kpts, mesh_kpts, mesh_shift):
    nbands, planes, points, width = path_bands.shape[1:]
    npath = lax.axis_size("path")
    nz = lax.axis_size("grid") // 2
    assert planes == 2 and nz == nbands and lax.axis_size("mesh") == 2
    half = points // 2
    share = nbands // 2
    forward_y, along_x, inverse_y, forward_z, inverse_z = tables(points)
    far_count, near_count, pitch = layout(points, nz)
    in_hbm = lambda array: pltpu.with_memory_space_constraint(array, pltpu.HBM)
    anywhere = pl.BlockSpec(memory_space=pl.ANY)
    vmem = lambda *shape: pltpu.VMEM(shape, F32)
    table = lambda array: pltpu.VMEM(array.shape, BF16)
    dma = lambda *shape: pltpu.SemaphoreType.DMA(shape)
    block = 2 * nbands // 4
    pairs = lambda *shape: [dma(*shape), dma(*shape)]
    scratch = [
        vmem(nz, 2, 2, points, width),
        vmem(far_count, near_count, 2, 2, points, width),
        vmem(points * pitch, width),
        vmem(nz, 2, 2, points, width),
        vmem(nz, 2, points, width),
        vmem(nz, points, width),
        vmem(nz, points, width),
        vmem(nz, points, width),
        vmem(nbands * points, width),
        vmem(share * points, width),
        vmem(nbands * 2 * points, width),
        table(forward_y[0]),
        table(along_x),
        table(inverse_y[0]),
        table(forward_z),
        table(inverse_z),
        vmem(points, width),
        vmem(share, 2 * nbands, width),
        vmem(nz, block, 128),
        vmem(4, block, 128),
        pltpu.SMEM(path_kpts.shape, jnp.int32),
        pltpu.SMEM(mesh_kpts.shape, jnp.int32),
        pltpu.SMEM(mesh_shift.shape, jnp.int32),
        dma(12),
        *pairs(far_count),
        *pairs(near_count),
        *pairs(1),
        *pairs(2, max(npath // 2, 1)),
        *pairs(npath),
        *pairs(nz),
        *pairs(nz),
        *pairs(2, nz),
        *pairs(1),
        *pairs(nz),
        *pairs(nz),
        *pairs(nz),
        *pairs(share),
        dma(2, share),
        *pairs(nz),
        *pairs(3),
    ]
    applied, inter = pl.pallas_call(
        functools.partial(body, points, nz, npath, nbands),
        name="exchange",
        out_shape=(
            jax.ShapeDtypeStruct((share * 2 * points, width), F32),
            jax.ShapeDtypeStruct((2 * nbands, nbands), F32),
        ),
        in_specs=[anywhere] * 10,
        out_specs=(anywhere, pl.BlockSpec(memory_space=pltpu.VMEM)),
        scratch_shapes=scratch,
        compiler_params=pltpu.CompilerParams(
            collective_id=0, has_side_effects=True, vmem_limit_bytes=40 << 20
        ),
    )(
        *map(
            in_hbm,
            (
                path_kpts,
                mesh_kpts,
                mesh_shift,
                path_bands.reshape(nbands * planes * points, width),
                occupied,
                jnp.asarray(forward_y),
                jnp.asarray(along_x),
                jnp.asarray(inverse_y),
                jnp.asarray(forward_z),
                jnp.asarray(inverse_z),
            ),
        )
    )
    return (
        applied.reshape(1, share, planes, points, width),
        inter.reshape(1, 2, nbands, nbands),
    )


def solution(mesh):
    return jax.shard_map(
        per_device,
        mesh=mesh,
        in_specs=(
            P("path", None, "grid", None, None),
            P("mesh", None, "grid", "path", None),
            P("path", None),
            P(),
            P(),
        ),
        out_specs=(P("path", "mesh", "grid", None, None), P("path", None, None, None)),
        check_vma=False,
    )
```

time: 139 us -> 124 us (0.89)
  local copies, waits for them, and re-layouts: 8.99 us -> 1.4 us
  Pallas kernels: 129 us -> 122 us
    unnamed x22 -> x2, local copies, waits for them, and re-layouts: 8.99 us -> 1.4 us
    pallas_call x1, Pallas kernels: 129 us -> 122 us  [per_device(): pl.pallas_call(functools.partial(body, points, nz, npath, nbands), name='...]
where the time goes in v2:
time: 124 us
  Pallas kernels  122 us (98%)
  local copies, waits for them, and re-layouts  1.4 us (1%)
    pallas_call x1, Pallas kernels, per_device(): pl.pallas_call(functools.partial(body, points, nz, npath, nbands), name='...  122 us

profile of v2, /device:TPU:1, one launch (start us, length us, event | category | flops | bytes accessed | tf_op | source)
XLA Modules:
  0.0 123.7 jit_solution(13576583605138651849)
XLA Ops:
  0.6 121.6 %exchange.1 = (f32[1024,128]{1,0:T(8,128)S(1)}, f32[32,16]{1,0:T(8,128)S(1)}) custom-call(s32[1,3]{1,0:T(1,128)} %kp_h.1, s32[2,3]{1,0:T(2,128)} %km_h.1, s32[2,3]{1,0:T(2,128)} %shift_h.1, f32[2048,128]{1,0:T(8,128)} %bitcast.5, f32[1,1,2,8,128]{4,3,2,1,0:T(8,128)} %occ.1, bf16[2,64,256]{2,1,0:T(8,128)(2,1)} %constant.10.clone.fy_h, ...), custom_call_target="tpu_custom_call" | custom-call | tf_op jit(solution)/shard_map/exchange/pallas_call | solution.py:601
  122.3 0.8 copy.14
  123.1 0.6 copy.15

commit v3 on v2

--- a/solution.py
+++ b/solution.py
@@ -66,7 +66,7 @@
     applied, inter,
     band_full, occ_full, field, part, core_in, y_out, y_in, z_out, z_in, relay_in, mine,
     fy, lx, iy, fz, iz, base, acc, pz, fin, kp, km, shift,
-    loc, of_s, of_r, on_s, on_r, oh_s, oh_r, ox_s, ox_r, oc_s, oc_r,
+    loc, on_s, on_r, oh_s, oh_r, ox_s, ox_r, oc_s, oc_r,
     bz_s, bz_r, by_s, by_r, bc_s, bc_r, bl_s, bl_r,
     rc_s, rc_r, ry_s, ry_r, rz_s, rz_r, rr_s, rr_r, out_s,
     ib_s, ib_r, ic_s, ic_r,
@@ -162,19 +162,11 @@
 
         lax.fori_loop(low, high, step, 0)
 
-    near_steps = [(1, -1, 2)[e] for e in range(near_count - 1)]
-
-    def occ_far_z(k, back=False):
-        at = lax.rem(far + (far_count - k if back else k), far_count)
-        spot = occ_full.at[at if back else far, near, c, :, my_rows, :]
+    def occ_z(i, back=False):
+        zz = source(i) if back else z
+        spot = occ_full.at[lax.div(zz, near_count), lax.rem(zz, near_count), c, :, my_rows, :]
         src = spot if back else occ.at[0, 0]
-        return remote(src, spot, of_s.at[k], of_r.at[k], ring(at * near_count + near))
-
-    def occ_near_z(k, back=False):
-        step = near_steps[k]
-        zz = lax.rem(z + nz - step if back else z + nz + step, nz)
-        spot = occ_full.at[:, lax.rem(zz, near_count) if back else near, c, :, my_rows, :]
-        return remote(spot, spot, on_s.at[k], on_r.at[k], ring(zz))
+        return remote(src, spot, on_s.at[i], on_r.at[i], ring(source(i) if back else target(i)))
 
     def band_z(i):
         dz = target(i)
@@ -222,24 +214,20 @@
         band_z_in(i).wait_recv()
         band_y(i, m).start()
         band_core(i, c, m, 0).start()
-        pl.when(i > 0)(lambda: late(i - 1))
+
+    def forward_and_late(i):
+        forward(i)
+        pl.when(i >= lag_y)(lambda: late(i - lag_y))
 
     steps = nz - 1
-    first_stop, second_stop, third_stop, fourth_stop = (
-        (4, 8, 9, 10) if nz == 16 else (1, steps, steps, steps)
-    )
-    for k in range(1, far_count):
-        occ_far_z(k).start()
-    each(0, second_stop, lambda i: band_z(i).start())
+    lag_y = 5 if nz == 16 else 1
+    first_stop, third_stop, fourth_stop = (4, 6, 10) if nz == 16 else (1, steps, steps)
+    each(0, steps, lambda i: occ_z(steps - 1 - i).start())
+    each(0, steps, lambda i: band_z(i).start())
     for copy in local[:3]:
         copy.wait()
     band_own(False).start()
-    each(0, first_stop, forward)
-    for k in range(1, far_count):
-        occ_far_z(k, True).wait_recv()
-    for k in range(near_count - 1):
-        occ_near_z(k).start()
-    each(second_stop, steps, lambda i: band_z(i).start())
+    each(0, first_stop, forward_and_late)
     for copy in local[3:]:
         copy.wait()
 
@@ -256,18 +244,17 @@
     freq_z = frequency(lane & (points - 1), 2)
     base[...] = scale * (freq_x * freq_x + freq_z * freq_z) + SCREEN_SQ
 
-    for k in range(near_count - 1):
-        occ_near_z(k, True).wait_recv()
+    each(0, steps, lambda i: occ_z(i, True).wait_recv())
     occ_far(path).start()
     for j in range(1, nx):
         occ_x(j, 0, path).start()
     occ_core(c, path).start()
-    each(first_stop, third_stop, forward)
+    each(first_stop, third_stop, forward_and_late)
     occ_far(far_path).wait_recv()
     for j in range(1, nx):
         occ_x(j, 1, far_path).start()
     occ_core(c, far_path).start()
-    each(third_stop, fourth_stop, forward)
+    each(third_stop, fourth_stop, forward_and_late)
     for which in range(2):
         for j in range(1, nx):
             side = hi_y if which == 0 else 1 - hi_y
@@ -333,7 +320,7 @@
         step = fourth_stop + lax.div(t, 3)
         turn = lax.rem(t, 3) == 0
         pl.when(turn & (step < steps))(lambda: forward(step))
-        pl.when(turn & (step == steps))(lambda: late(steps - 1))
+        pl.when((t >= fourth_stop - lag_y) & (t < steps))(lambda: late(t))
 
         def fetched():
             band_core(t - 1, other_c, m, 0).wait_recv()
@@ -345,7 +332,7 @@
 
     each(0, nz, first_phase)
 
-    batch = min(4, half)
+    batch = min(8, half)
 
     def second_phase(t):
         spots, tiles, kernels = [], [], []
@@ -365,8 +352,17 @@
 
     each(0, half // batch, second_phase)
 
+    def offset_back(i):
+        return (nz // 2 - lax.div(i + 1, 2)) * (2 * lax.rem(i, 2) - 1)
+
+    def target_back(i):
+        return lax.rem(z + offset_back(i) + nz, nz)
+
+    def source_back(i):
+        return lax.rem(z - offset_back(i) + nz, nz)
+
     def restore(i):
-        zz = target(i)
+        zz = target_back(i)
         values = along_z(
             iz[...], jnp.concatenate([field[x_rows(zz, t), :] for t in range(4)], 0)
         )
@@ -383,11 +379,11 @@
         return remote(y_out.at[i], y_in.at[i], ry_s.at[i], ry_r.at[i], y_peer)
 
     def give_z(i):
-        return remote(z_out.at[i], z_in.at[slab(z)], rz_s.at[i], rz_r.at[i], ring(target(i)))
+        return remote(z_out.at[i], z_in.at[slab(z)], rz_s.at[i], rz_r.at[i], ring(target_back(i)))
 
     def give_z_in(i):
-        spot = z_in.at[slab(source(i))]
-        return remote(spot, spot, rz_s.at[i], rz_r.at[i], ring(source(i)))
+        spot = z_in.at[slab(source_back(i))]
+        return remote(spot, spot, rz_s.at[i], rz_r.at[i], ring(source_back(i)))
 
     def over_cores(i):
         give_core(i).wait_recv()
@@ -457,15 +453,15 @@
 
     def arrive(i):
         pl.when(i > 0)(lambda: give_z_in(i - 1).wait_recv())
-        pl.when(i < nz)(lambda: settle(source(jnp.where(i == 0, nz - 1, i - 1))))
-
-    lag_relay = 2
+        pl.when(i < nz)(lambda: settle(source_back(jnp.where(i == 0, nz - 1, i - 1))))
+
+    lag_relay = 5 if nz == 16 else 2
 
     def arrive_step(i):
         pl.when(i < nz)(lambda: arrive(i))
         before = i - lag_relay
         pl.when(before >= 0)(
-            lambda: relayed(source(jnp.where(before == 0, nz - 1, before - 1)))
+            lambda: relayed(source_back(jnp.where(before == 0, nz - 1, before - 1)))
         )
 
     each(0, nz + lag_relay, arrive_step)
@@ -515,10 +511,7 @@
         turned_tile = result if group == 0 else pltpu.roll(result, 128 - group * nbands, 1)
         inter[group * block : (group + 1) * block, :] = turned_tile[:, :nbands]
 
-    for k in range(1, far_count):
-        occ_far_z(k).wait_send()
-    for k in range(near_count - 1):
-        occ_near_z(k).wait_send()
+    each(0, steps, lambda i: occ_z(i).wait_send())
     each(0, steps, lambda i: band_z(i).wait_send())
     band_own(False).wait_send()
     occ_far(path).wait_send()
@@ -581,8 +574,7 @@
         pltpu.SMEM(mesh_kpts.shape, jnp.int32),
         pltpu.SMEM(mesh_shift.shape, jnp.int32),
         dma(12),
-        *pairs(far_count),
-        *pairs(near_count),
+        *pairs(nz),
         *pairs(1),
         *pairs(2, max(npath // 2, 1)),
         *pairs(npath),

time: 124 us -> 110 us (0.89)
  Pallas kernels: 122 us -> 107 us
    pallas_call x1, Pallas kernels: 122 us -> 107 us  [per_device(): pl.pallas_call(functools.partial(body, points, nz, npath, nbands), name='...]
where the time goes in v3:
time: 110 us; the launch traced here: 109 us
  Pallas kernels  107 us (97%)
  local copies, waits for them, and re-layouts  1.4 us (1%)
    pallas_call x1, Pallas kernels, per_device(): pl.pallas_call(functools.partial(body, points, nz, npath, nbands), name='...  107 us

profile of v3, /device:TPU:1, one launch (start us, length us, event | category | flops | bytes accessed | tf_op | source)
XLA Modules:
  0.0 109.4 jit_solution(604308921953948046)
XLA Ops:
  0.6 107.3 %exchange.1 = (f32[1024,128]{1,0:T(8,128)S(1)}, f32[32,16]{1,0:T(8,128)S(1)}) custom-call(s32[1,3]{1,0:T(1,128)} %kp_h.1, s32[2,3]{1,0:T(2,128)} %km_h.1, s32[2,3]{1,0:T(2,128)} %shift_h.1, f32[2048,128]{1,0:T(8,128)} %bitcast.5, f32[1,1,2,8,128]{4,3,2,1,0:T(8,128)} %occ.1, bf16[2,64,256]{2,1,0:T(8,128)(2,1)} %constant.10.clone.fy_h, ...), custom_call_target="tpu_custom_call" | custom-call | tf_op jit(solution)/shard_map/exchange/pallas_call | solution.py:593
  108.0 0.8 copy.14
  108.8 0.6 copy.15

commit v4 on v3

--- a/solution.py
+++ b/solution.py
@@ -221,7 +221,7 @@
 
     steps = nz - 1
     lag_y = 5 if nz == 16 else 1
-    first_stop, third_stop, fourth_stop = (4, 6, 10) if nz == 16 else (1, steps, steps)
+    first_stop, third_stop, fourth_stop = (4, 6, 12) if nz == 16 else (1, steps, steps)
     each(0, steps, lambda i: occ_z(steps - 1 - i).start())
     each(0, steps, lambda i: band_z(i).start())
     for copy in local[:3]:
@@ -305,34 +305,43 @@
     def x_rows(zz, t):
         return pl.ds(pl.multiple_of((zz * 4 + t) * pitch, 8), half)
 
-    def transform(zz):
+    def transform(sources):
         tiles = []
-        for t in range(4):
-            band = band_full[zz, t // 2, t % 2]
-            even, odd = factors(orbital(zz, t // 2, t % 2))
-            tiles.append(even * band + odd * swap(band))
+        for zz in sources:
+            for t in range(4):
+                band = band_full[zz, t // 2, t % 2]
+                even, odd = factors(orbital(zz, t // 2, t % 2))
+                tiles.append(even * band + odd * swap(band))
         summed = [forward_sum(pair) for pair in contract(fy[...], tiles)]
         values = along_z(fz[...], jnp.concatenate(summed, 0))
-        for t in range(4):
-            field[x_rows(zz, t), :] = values[t * half : (t + 1) * half]
+        for t in range(4 * len(sources)):
+            field[x_rows(sources[t // 4], t % 4), :] = values[t * half : (t + 1) * half]
+
+    group = 4
 
     def first_phase(t):
-        step = fourth_stop + lax.div(t, 3)
-        turn = lax.rem(t, 3) == 0
-        pl.when(turn & (step < steps))(lambda: forward(step))
-        pl.when((t >= fourth_stop - lag_y) & (t < steps))(lambda: late(t))
-
-        def fetched():
-            band_core(t - 1, other_c, m, 0).wait_recv()
-            band_core(t - 1, other_c, other_m, 1).wait_recv()
-
-        pl.when(t > 0)(fetched)
+        step = fourth_stop + t
+        pl.when(step < steps)(lambda: forward(step))
+        for k in range(group):
+            ahead = group * t + group - 1 + k
+            pl.when((ahead >= fourth_stop - lag_y) & (ahead < steps))(
+                functools.partial(late, ahead)
+            )
+
+        def fetched(i):
+            band_core(i, other_c, m, 0).wait_recv()
+            band_core(i, other_c, other_m, 1).wait_recv()
+
         pl.when(t == 0)(lambda: band_own(True).wait_recv())
-        transform(source(jnp.where(t == 0, nz - 1, t - 1)))
-
-    each(0, nz, first_phase)
-
-    batch = min(8, half)
+        pl.when(t > 0)(lambda: fetched(group * t - 1))
+        for k in range(1, group):
+            fetched(group * t + k - 1)
+        first = source(jnp.where(t == 0, nz - 1, group * t - 1))
+        transform([first] + [source(group * t + k - 1) for k in range(1, group)])
+
+    each(0, nz // group, first_phase)
+
+    batch = min(16, half)
 
     def second_phase(t):
         spots, tiles, kernels = [], [], []

time: 110 us -> 105 us (0.955)
  Pallas kernels: 107 us -> 103 us
    pallas_call x1, Pallas kernels: 107 us -> 103 us  [per_device(): pl.pallas_call(functools.partial(body, points, nz, npath, nbands), name='...]
where the time goes in v4:
time: 105 us
  Pallas kernels  103 us (98%)
  local copies, waits for them, and re-layouts  1.4 us (1%)
    pallas_call x1, Pallas kernels, per_device(): pl.pallas_call(functools.partial(body, points, nz, npath, nbands), name='...  103 us

profile of v4, /device:TPU:1, one launch (start us, length us, event | category | flops | bytes accessed | tf_op | source)
XLA Modules:
  0.0 104.7 jit_solution(17167497581738775903)
XLA Ops:
  0.6 102.7 %exchange.1 = (f32[1024,128]{1,0:T(8,128)S(1)}, f32[32,16]{1,0:T(8,128)S(1)}) custom-call(s32[1,3]{1,0:T(1,128)} %kp_h.1, s32[2,3]{1,0:T(2,128)} %km_h.1, s32[2,3]{1,0:T(2,128)} %shift_h.1, f32[2048,128]{1,0:T(8,128)} %bitcast.5, f32[1,1,2,8,128]{4,3,2,1,0:T(8,128)} %occ.1, bf16[2,64,256]{2,1,0:T(8,128)(2,1)} %constant.10.clone.fy_h, ...), custom_call_target="tpu_custom_call" | custom-call | tf_op jit(solution)/shard_map/exchange/pallas_call | solution.py:602
  103.3 0.8 copy.14
  104.1 0.6 copy.15

commit v5 on v4

--- a/solution.py
+++ b/solution.py
@@ -221,7 +221,7 @@
 
     steps = nz - 1
     lag_y = 5 if nz == 16 else 1
-    first_stop, third_stop, fourth_stop = (4, 6, 12) if nz == 16 else (1, steps, steps)
+    first_stop, third_stop, fourth_stop = (2, 4, 13) if nz == 16 else (1, steps, steps)
     each(0, steps, lambda i: occ_z(steps - 1 - i).start())
     each(0, steps, lambda i: band_z(i).start())
     for copy in local[:3]:
@@ -464,7 +464,7 @@
         pl.when(i > 0)(lambda: give_z_in(i - 1).wait_recv())
         pl.when(i < nz)(lambda: settle(source_back(jnp.where(i == 0, nz - 1, i - 1))))
 
-    lag_relay = 5 if nz == 16 else 2
+    lag_relay = 8 if nz == 16 else 2
 
     def arrive_step(i):
         pl.when(i < nz)(lambda: arrive(i))

time: 105 us -> 104 us (level)
  no operation moved by 1% of the time
where the time goes in v5:
time: 104 us
  Pallas kernels  102 us (98%)
  local copies, waits for them, and re-layouts  1.4 us (1%)
    pallas_call x1, Pallas kernels, per_device(): pl.pallas_call(functools.partial(body, points, nz, npath, nbands), name='...  102 us

profile of v5, /device:TPU:1, one launch (start us, length us, event | category | flops | bytes accessed | tf_op | source)
XLA Modules:
  0.0 104.3 jit_solution(15806671372243679405)
XLA Ops:
  0.6 102.3 %exchange.1 = (f32[1024,128]{1,0:T(8,128)S(1)}, f32[32,16]{1,0:T(8,128)S(1)}) custom-call(s32[1,3]{1,0:T(1,128)} %kp_h.1, s32[2,3]{1,0:T(2,128)} %km_h.1, s32[2,3]{1,0:T(2,128)} %shift_h.1, f32[2048,128]{1,0:T(8,128)} %bitcast.5, f32[1,1,2,8,128]{4,3,2,1,0:T(8,128)} %occ.1, bf16[2,64,256]{2,1,0:T(8,128)(2,1)} %constant.10.clone.fy_h, ...), custom_call_target="tpu_custom_call" | custom-call | tf_op jit(solution)/shard_map/exchange/pallas_call | solution.py:602
  102.9 0.8 copy.14
  103.7 0.6 copy.15
